TPU v7x, 32 devices: a whole 2x2x4 slice. The times are simulated.
32 devices in a mesh: freq: 4 (over x, core), gblk: 8 (over z, y).
Axes of the slice: x: 2, y: 2, z: 4, core: 2. Of those that a mesh axis runs over, the one named last changes fastest.
Arguments:
- w_imag: bfloat16 [8, 8192, 16384], P('freq', 'gblk'), may hold values from -0.046875 to 0.046875
- w_real: bfloat16 [4, 8192, 16384], P('freq', 'gblk'), may hold values from -0.046875 to 0.046875
- pair_elements: bfloat16 [8192, 256], P('gblk'), may hold values from -0.75 to 0.75
- quad_weight: float32 [8, 128], P('freq'), may hold values from 0.1 to 1
- residue_freq: int32 [128], replicated, may hold values from 0 to 3
- owner_bands: int32 [128], replicated, may hold values from 0 to 127, each once
Outputs:
- sigma: float32 [128, 256], P(('freq', 'gblk'))
Inputs may be any that keep to these rules, and one draw needn't show every extreme that they name: `owner_bands`: each band appears once.
All inputs are finite; a program needn't handle non-finite values.
Results may differ from a plain program's by a relative error of at most 0.0003.
Values may be sent and summed in bfloat16 or wider, within the bound.
A program may use at most 192 MiB of HBM per device.

v0:
```python
import jax
import jax.numpy as jnp
from jax import lax
from jax.sharding import PartitionSpec as P


def on_device(w_imag, w_real, pair_elements, quad_weight, residue_freq, owner_bands):
    bands = pair_elements.shape[1] // 2
    g_count = w_imag.shape[2] // 2
    fr_local = w_real.shape[0]
    wide_elems = pair_elements.astype(jnp.float32)
    freq_first_index = lax.axis_index("freq") * fr_local
    real_ids = freq_first_index + jnp.arange(fr_local, dtype=jnp.int32)
    residue_weight = (residue_freq[None, :] == real_ids[:, None]).astype(jnp.float32)
    shard_rows = lax.all_gather(pair_elements, "gblk", axis=0, tiled=True)
    row_span = shard_rows.shape[0]
    lower_rows = jnp.concatenate([-shard_rows[:, bands:], shard_rows[:, :bands]], axis=1)

    def contrib(matrix):
        upper_cols = lax.slice_in_dim(matrix, 0, row_span, axis=2)
        lower_cols = lax.dynamic_slice_in_dim(matrix, g_count, row_span, 2)
        result = jnp.einsum(
            "frg,gc->frc", upper_cols, shard_rows, preferred_element_type=jnp.float32
        )
        return result + jnp.einsum(
            "frg,gc->frc", lower_cols, lower_rows, preferred_element_type=jnp.float32
        )

    x_imag = contrib(w_imag)
    x_real = contrib(w_real)

    def sandwich(products):
        blocks = jnp.einsum("gb,fgc->fbc", wide_elems, products, precision=lax.Precision.HIGHEST)
        sig_re = blocks[:, :bands, :bands] + blocks[:, bands:, bands:]
        sig_im = blocks[:, :bands, bands:] - blocks[:, bands:, :bands]
        return jnp.concatenate([sig_re, sig_im], axis=2)

    partial_value = jnp.sum(quad_weight[:, :, None] * sandwich(x_imag), axis=0)
    partial_value = partial_value + jnp.sum(residue_weight[:, :, None] * sandwich(x_real), axis=0)
    onehot = (owner_bands[:, None] == jnp.arange(bands, dtype=jnp.int32)[None, :]).astype(
        jnp.float32
    )
    permuted = jnp.dot(onehot, partial_value, precision=lax.Precision.HIGHEST)
    grouped = lax.psum_scatter(permuted, "freq", scatter_dimension=0, tiled=True)
    sigma = lax.psum_scatter(grouped, "gblk", scatter_dimension=0, tiled=True)
    return sigma


def solution(mesh):
    placed = (
        P("freq", "gblk", None),
        P("freq", "gblk", None),
        P("gblk", None),
        P("freq", None),
        P(),
        P(),
    )
    return jax.shard_map(
        on_device, mesh=mesh, in_specs=placed, out_specs=P(("freq", "gblk"), None), check_vma=False
    )
```

profile of v0, /device:TPU:0, one launch (start us, length us, event | category | flops | bytes accessed | tf_op | source)
XLA Modules:
  0.0 208.3 jit_solution(6413655461911375520)
XLA Ops:
  6.5 0.0 all-gather.2.cloned.1.call-start
  6.5 0.7 all-gather.2.cloned.1.call-update
  7.3 0.0 reduce-scatter.2.cloned.1.call-start
  7.3 0.7 compare_convert_fusion
  8.0 77.0 %all-gather.2.cloned.1.call-done = bf16[8192,256]{1,0:T(8,128)(2,1)} async-done(((bf16[1024,256]{1,0:T(8,128)(2,1)}), bf16[8192,256]{1,0:T(8,128)(2,1)}) %all-gather.2.cloned.1.call-update) | async-done | bytes 4194320 | tf_op jit(solution)/shard_map/all_gather | solution.py:15
  85.0 0.0 copy-start.1
  85.0 2.8 %slice_negate_fusion = (bf16[8192,128]{1,0:T(8,128)(2,1)S(1)}, bf16[8192,128]{1,0:T(8,128)(2,1)S(1)}) fusion(bf16[8192,256]{1,0:T(8,128)(2,1)} %all-gather.2.cloned.1.call-done), kind=kLoop, calls=%fused_computation.13 | loop fusion | flops 1048576 | bytes 8388608 | tf_op jit(solution)/shard_map/neg | solution.py:17
  87.8 0.7 copy-done.1
  88.5 0.0 copy-start.2
  88.5 0.0 copy-start.3
  88.5 9.6 %fusion.6 = f32[1024,256]{1,0:T(8,128)S(1)} fusion(bf16[8192,256]{1,0:T(8,128)(2,1)S(1)} %copy-done.1, bf16[1,1024,16384]{2,1,0:T(8,128)(2,1)} %param.7), kind=kOutput, calls=%fused_computation.6 | convolution fusion | flops 4294967296 | bytes 22020096 | tf_op jit(solution)/shard_map/frg,gc->frc/dot_general | solution.py:22
  98.1 0.0 copy-done.2
  98.1 0.0 copy-done.3
  98.1 11.3 %fusion.16 = f32[1024,256]{1,0:T(8,128)} fusion(f32[1024,256]{1,0:T(8,128)S(1)} %fusion.6, bf16[8192,128]{1,0:T(8,128)(2,1)S(1)} %get-tuple-element.6, bf16[8192,128]{1,0:T(8,128)(2,1)S(1)} %get-tuple-element.5, bf16[1,1024,16384]{2,1,0:T(8,128)(2,1)} %param.7), kind=kOutput, calls=%fused_computation.17 | convolution fusion | flops 4303618048 | bytes 23068672 | tf_op jit(solution)/shard_map/frg,gc->frc/dot_general | solution.py:25
  109.4 0.0 copy-start
  109.4 15.4 %fusion = f32[256,2,1024]{2,0,1:T(8,128)S(1)} fusion(bf16[2,1024,16384]{2,1,0:T(8,128)(2,1)} %param.6, bf16[8192,128]{1,0:T(8,128)(2,1)} %copy-done.3, bf16[8192,128]{1,0:T(8,128)(2,1)} %copy-done.2), kind=kOutput, calls=%fused_computation | convolution fusion | flops 8598323200 | bytes 39845888 | tf_op jit(solution)/shard_map/frg,gc->frc/dot_general | solution.py:25
  124.9 0.0 copy-done
  124.9 2.2 %convolution_bitcast_fusion = f32[1,256,256]{1,2,0:T(8,128)S(1)} fusion(f32[1024,256]{1,0:T(8,128)} %fusion.16, bf16[1024,256]{1,0:T(8,128)(2,1)S(1)} %copy-done), kind=kOutput, calls=%fused_computation.19 | convolution fusion | flops 805306368 | bytes 1835008 | tf_op jit(solution)/shard_map/gb,fgc->fbc/dot_general | solution.py:33
  127.1 15.4 %fusion.2 = f32[2,1024,256]{1,2,0:T(8,128)S(1)} fusion(bf16[2,1024,16384]{2,1,0:T(8,128)(2,1)} %param.6, bf16[8192,256]{1,0:T(8,128)(2,1)} %all-gather.2.cloned.1.call-done), kind=kOutput, calls=%fused_computation.2 | convolution fusion | flops 8589934592 | bytes 39845888 | tf_op jit(solution)/shard_map/frg,gc->frc/dot_general | solution.py:22
  142.5 0.0 copy-start.4
  142.5 0.0 copy-start.5
  142.6 0.0 copy-start.6
  142.6 1.2 fusion.19
  143.8 0.0 copy-done.4
  143.9 0.0 copy-done.5
  143.9 0.9 fusion.23
  144.8 0.0 reduce-scatter.2.cloned.1.call-update
  144.8 0.0 copy-done.6
  144.8 0.6 dynamic-slice
  146.1 17.1 %reduce-scatter.2.cloned.1.call-done = f32[32,256]{1,0:T(8,128)} async-done(((f32[128,256]{1,0:T(8,128)}), f32[32,256]{1,0:T(8,128)}) %reduce-scatter.2.cloned.1.call-update) | async-done | bytes 32784 | tf_op jit(solution)/shard_map/reduce_scatter | solution.py:44
  163.1 37.8 %all-reduce = f32[32,256]{1,0:T(8,128)S(1)} all-reduce(f32[32,256]{1,0:T(8,128)} %reduce-scatter.2.cloned.1.call-done), channel_id=3, replica_groups=mesh['freq'=4,'gblk'=8] {'gblk'}, use_global_device_ids=true, to_apply=%region_2.0.clone | all-reduce | flops 8192 | bytes 65536
  200.9 0.6 constant_dynamic-slice_fusion
  (3 shorter events, 0.1 us)
Async XLA Ops:
  6.5 78.5 %all-gather.2.cloned.1.call-start = ((), (), s32[]{:S(2)}) async-start(), calls=%async_computation.1 | async-start | bytes 4718592 | tf_op jit(solution)/shard_map/all_gather | solution.py:15
  7.3 155.9 %reduce-scatter.2.cloned.1.call-start = ((), (), s32[]{:S(2)}) async-start(), calls=%async_computation.2 | async-start | bytes 163840 | tf_op jit(solution)/shard_map/reduce_scatter | solution.py:44
  85.0 3.4 %copy-start.1 = (bf16[8192,256]{1,0:T(8,128)(2,1)S(1)}, bf16[8192,256]{1,0:T(8,128)(2,1)}, u32[]{:S(2)}) copy-start(bf16[8192,256]{1,0:T(8,128)(2,1)} %all-gather.2.cloned.1.call-done) | copy-start | bytes 12582916
  88.5 9.6 %copy-start.2 = (bf16[8192,128]{1,0:T(8,128)(2,1)}, bf16[8192,128]{1,0:T(8,128)(2,1)S(1)}, u32[]{:S(2)}) copy-start(bf16[8192,128]{1,0:T(8,128)(2,1)S(1)} %get-tuple-element.5) | copy-start | bytes 6291460
  88.5 9.7 %copy-start.3 = (bf16[8192,128]{1,0:T(8,128)(2,1)}, bf16[8192,128]{1,0:T(8,128)(2,1)S(1)}, u32[]{:S(2)}) copy-start(bf16[8192,128]{1,0:T(8,128)(2,1)S(1)} %get-tuple-element.6) | copy-start | bytes 6291460
  109.4 15.5 %copy-start = (bf16[1024,256]{1,0:T(8,128)(2,1)S(1)}, bf16[1024,256]{1,0:T(8,128)(2,1)}, u32[]{:S(2)}) copy-start(bf16[1024,256]{1,0:T(8,128)(2,1)} %param.8) | copy-start | bytes 1572868
  142.5 1.3 copy-start.4
  142.5 1.3 copy-start.5
  142.6 2.3 %copy-start.6 = (u32[32]{0:T(128)S(1)}, u32[32]{0:T(128)}, u32[]{:S(2)}) copy-start(u32[32]{0:T(128)} %constant.12) | copy-start | bytes 388
Sparse Core Ops, SparseCore 0:
  9.5 75.5 all-gather.1
  144.9 18.1 reduce-scatter.1
where the time goes:
time: 209 us; the launch traced here: 208 us
  waiting for transfers between devices  94.8 us (45%)
  matrix products  56.1 us (27%)
  blocking collectives  37.8 us (18%)
  between operations  14.2 us (7%)
  other arithmetic  3.5 us (2%)
    all_gather x1, waiting for transfers between devices, on_device(): shard_rows = lax.all_gather(pair_elements, 'gblk', axis=0, tiled=True)  77 us
    unnamed x1, blocking collectives  37.8 us
    dot_general x2, matrix products, contrib(): jnp.einsum('frg,gc->frc', lower_cols, lower_rows, preferred_element_type=...  26.8 us
    dot_general x2, matrix products, contrib(): jnp.einsum('frg,gc->frc', upper_cols, shard_rows, preferred_element_type=...  25 us
    reduce_scatter x1, waiting for transfers between devices, on_device(): lax.psum_scatter(permuted, 'freq', scatter_dimension=0, tiled=True)  17.1 us
  transfers between devices with their start and end apart: 2, of which 2 were waited for; matrix products, arithmetic and copies ran while one was open for 1% of the time, Pallas kernels for 0%

commit v1 on v0

--- a/solution.py
+++ b/solution.py
@@ -12,7 +12,12 @@
     freq_first_index = lax.axis_index("freq") * fr_local
     real_ids = freq_first_index + jnp.arange(fr_local, dtype=jnp.int32)
     residue_weight = (residue_freq[None, :] == real_ids[:, None]).astype(jnp.float32)
-    shard_rows = lax.all_gather(pair_elements, "gblk", axis=0, tiled=True)
+    ring = [pair_elements]
+    for hop in range(7):
+        ring.append(lax.ppermute(ring[-1], "gblk", [(dev, (dev + 1) % 8) for dev in range(8)]))
+    shard_rows = jnp.roll(
+        jnp.concatenate(ring[::-1], axis=0), (lax.axis_index("gblk") + 1) * ring[0].shape[0], axis=0
+    )
     row_span = shard_rows.shape[0]
     lower_rows = jnp.concatenate([-shard_rows[:, bands:], shard_rows[:, :bands]], axis=1)
 

time: 209 us -> 242 us (1.16)
  waiting for transfers between devices: 94.8 us -> 113 us
  matrix products: 56.1 us -> 63.7 us
  local copies, waits for them, and re-layouts: 1.88 us -> 6.99 us
  starting transfers between devices: 0.04 us -> 3.01 us
    ppermute x0 -> x7, waiting for transfers between devices: none -> 97.2 us  [on_device(): lax.ppermute(ring[-1], 'gblk', [(dev, (dev + 1) % 8) for dev in range(8)])]
    all_gather x1 -> x0, waiting for transfers between devices: 77 us -> none  [on_device(): shard_rows = lax.all_gather(pair_elements, 'gblk', axis=0, tiled=True)]
    unnamed x16 -> x29, local copies, waits for them, and re-layouts: 1.88 us -> 6.95 us
    dot_general x2, matrix products: 25 us -> 29.6 us  [contrib(): jnp.einsum('frg,gc->frc', upper_cols, shard_rows, preferred_element_type=...]
    ppermute x0 -> x7, starting transfers between devices: none -> 3.01 us  [on_device(): lax.ppermute(ring[-1], 'gblk', [(dev, (dev + 1) % 8) for dev in range(8)])]
  transfers between devices with their start and end apart: 2 -> 8, of which waited for: 2 -> 8; matrix products, arithmetic and copies ran while one was open for 1% -> 1% of each run, Pallas kernels for 0% -> 0%
where the time goes in v1:
time: 242 us; the launch traced here: 241 us
  waiting for transfers between devices  113 us (47%)
  matrix products  63.7 us (26%)
  blocking collectives  37.8 us (16%)
  between operations  14.3 us (6%)
  local copies, waits for them, and re-layouts  6.99 us (3%)
  other arithmetic  3.12 us (1%)
  starting transfers between devices  3.01 us (1%)
    ppermute x7, waiting for transfers between devices, on_device(): lax.ppermute(ring[-1], 'gblk', [(dev, (dev + 1) % 8) for dev in range(8)])  97.2 us
    unnamed x1, blocking collectives  37.8 us
    dot_general x2, matrix products, contrib(): jnp.einsum('frg,gc->frc', upper_cols, shard_rows, preferred_element_type=...  29.6 us
    dot_general x2, matrix products, contrib(): jnp.einsum('frg,gc->frc', lower_cols, lower_rows, preferred_element_type=...  28.6 us
    reduce_scatter x1, waiting for transfers between devices, on_device(): lax.psum_scatter(permuted, 'freq', scatter_dimension=0, tiled=True)  15.3 us
    unnamed x29, local copies, waits for them, and re-layouts  6.95 us
  transfers between devices with their start and end apart: 8, of which 8 were waited for; matrix products, arithmetic and copies ran while one was open for 1% of the time, Pallas kernels for 0%

profile of v1, /device:TPU:0, one launch (start us, length us, event | category | flops | bytes accessed | tf_op | source)
XLA Modules:
  0.0 241.4 jit_solution(9872363299791154835)
XLA Ops:
  6.5 0.0 copy-start
  6.5 0.0 reduce-scatter.2.cloned.1.call-start
  6.5 3.0 %collective-permute-start = (bf16[1024,256]{1,0:T(8,128)(2,1)}, bf16[1024,256]{1,0:T(8,128)(2,1)S(1)}, u32[]{:S(2)}, u32[]{:S(2)}) collective-permute-start(bf16[1024,256]{1,0:T(8,128)(2,1)} %param.8), channel_id=1, source_target_pairs={{0,1},{1,2},{2,3},{3,4},{4,5},{5,6},{6,7},{7,0},{8,9},{9,10},{10,1... | collective-permute-start | bytes 1572872 | tf_op jit(solution)/shard_map/ppermute | solution.py:17
  9.5 15.2 %collective-permute-done = bf16[1024,256]{1,0:T(8,128)(2,1)S(1)} collective-permute-done((bf16[1024,256]{1,0:T(8,128)(2,1)}, bf16[1024,256]{1,0:T(8,128)(2,1)S(1)}, u32[]{:S(2)}, u32[]{:S(2)}) %collective-permute-start) | collective-permute-done | bytes 524320 | tf_op jit(solution)/shard_map/ppermute | solution.py:17
  24.8 0.0 collective-permute-start.1
  24.8 15.8 %collective-permute-done.1 = bf16[1024,256]{1,0:T(8,128)(2,1)S(1)} collective-permute-done((bf16[1024,256]{1,0:T(8,128)(2,1)S(1)}, bf16[1024,256]{1,0:T(8,128)(2,1)S(1)}, u32[]{:S(2)}, u32[]{:S(2)}) %collective-permute-start.1) | collective-permute-done | bytes 524320 | tf_op jit(solution)/shard_map/ppermute | solution.py:17
  40.6 0.0 collective-permute-start.2
  40.6 14.9 %collective-permute-done.2 = bf16[1024,256]{1,0:T(8,128)(2,1)S(1)} collective-permute-done((bf16[1024,256]{1,0:T(8,128)(2,1)S(1)}, bf16[1024,256]{1,0:T(8,128)(2,1)S(1)}, u32[]{:S(2)}, u32[]{:S(2)}) %collective-permute-start.2) | collective-permute-done | bytes 524320 | tf_op jit(solution)/shard_map/ppermute | solution.py:17
  55.5 0.0 collective-permute-start.3
  55.5 14.1 %collective-permute-done.3 = bf16[1024,256]{1,0:T(8,128)(2,1)S(1)} collective-permute-done((bf16[1024,256]{1,0:T(8,128)(2,1)S(1)}, bf16[1024,256]{1,0:T(8,128)(2,1)S(1)}, u32[]{:S(2)}, u32[]{:S(2)}) %collective-permute-start.3) | collective-permute-done | bytes 524320 | tf_op jit(solution)/shard_map/ppermute | solution.py:17
  69.6 0.0 collective-permute-start.4
  69.6 13.2 %collective-permute-done.4 = bf16[1024,256]{1,0:T(8,128)(2,1)S(1)} collective-permute-done((bf16[1024,256]{1,0:T(8,128)(2,1)S(1)}, bf16[1024,256]{1,0:T(8,128)(2,1)S(1)}, u32[]{:S(2)}, u32[]{:S(2)}) %collective-permute-start.4) | collective-permute-done | bytes 524320 | tf_op jit(solution)/shard_map/ppermute | solution.py:17
  82.8 0.0 collective-permute-start.5
  82.8 12.5 %collective-permute-done.5 = bf16[1024,256]{1,0:T(8,128)(2,1)} collective-permute-done((bf16[1024,256]{1,0:T(8,128)(2,1)S(1)}, bf16[1024,256]{1,0:T(8,128)(2,1)}, u32[]{:S(2)}, u32[]{:S(2)}) %collective-permute-start.5) | collective-permute-done | bytes 524320 | tf_op jit(solution)/shard_map/ppermute | solution.py:17
  95.2 0.0 collective-permute-start.6
  95.3 0.7 compare_convert_fusion
  95.9 11.5 %collective-permute-done.6 = bf16[1024,256]{1,0:T(8,128)(2,1)} collective-permute-done((bf16[1024,256]{1,0:T(8,128)(2,1)}, bf16[1024,256]{1,0:T(8,128)(2,1)}, u32[]{:S(2)}, u32[]{:S(2)}) %collective-permute-start.6) | collective-permute-done | bytes 524320 | tf_op jit(solution)/shard_map/ppermute | solution.py:17
  107.4 1.1 constant_dynamic-update-slice_fusion.15
  108.5 1.1 constant_dynamic-update-slice_fusion.14
  109.8 1.1 constant_dynamic-update-slice_fusion.8
  110.9 1.1 constant_dynamic-update-slice_fusion.7
  112.0 1.1 constant_dynamic-update-slice_fusion.6
  113.3 0.0 copy-done
  113.3 0.0 copy-start.1
  113.4 2.4 dynamic-slice_negate_fusion
  115.7 16.7 %fusion.2 = f32[256,2,1024]{2,0,1:T(8,128)} fusion(bf16[2,1024,16384]{2,1,0:T(8,128)(2,1)} %param.6, bf16[16384,256]{1,0:T(8,128)(2,1)S(1)} %constant_dynamic-update-slice_fusion, s32[]{:T(128)S(6)} %select_n.14), kind=kOutput, calls=%fused_computation.2 | convolution fusion | flops 8589934592 | bytes 39845892 | tf_op jit(solution)/shard_map/frg,gc->frc/dot_general | solution.py:27
  132.4 0.0 copy-done.1
  132.4 16.7 %fusion = f32[256,2,1024]{2,0,1:T(8,128)} fusion(bf16[2,1024,16384]{2,1,0:T(8,128)(2,1)} %param.6, bf16[8192,128]{1,0:T(8,128)(2,1)} %get-tuple-element.6, bf16[8192,128]{1,0:T(8,128)(2,1)S(1)} %get-tuple-element.5), kind=kOutput, calls=%fused_computation | convolution fusion | flops 8598323200 | bytes 39845888 | tf_op jit(solution)/shard_map/frg,gc->frc/dot_general | solution.py:30
  149.1 11.9 %fusion.4 = f32[256,1024]{1,0:T(8,128)} fusion(bf16[1,1024,16384]{2,1,0:T(8,128)(2,1)} %param.7, bf16[8192,128]{1,0:T(8,128)(2,1)} %get-tuple-element.6, bf16[8192,128]{1,0:T(8,128)(2,1)S(1)} %get-tuple-element.5), kind=kOutput, calls=%fused_computation.4 | convolution fusion | flops 4303355904 | bytes 22020096 | tf_op jit(solution)/shard_map/frg,gc->frc/dot_general | solution.py:30
  161.0 0.0 copy-start.2
  161.0 0.0 copy-start.3
  161.0 12.9 %fusion.17 = f32[256,1024]{1,0:T(8,128)} fusion(f32[256,1024]{1,0:T(8,128)} %fusion.4, bf16[1,1024,16384]{2,1,0:T(8,128)(2,1)} %param.7, bf16[16384,256]{1,0:T(8,128)(2,1)} %copy-done.1, s32[]{:T(128)S(6)} %select_n.14), kind=kOutput, calls=%fused_computation.19 | convolution fusion | flops 4295229440 | bytes 23068676 | tf_op jit(solution)/shard_map/frg,gc->frc/dot_general | solution.py:27
  173.9 0.0 copy-start.4
  173.9 0.0 copy-start.5
  173.9 1.9 convolution_bitcast_fusion
  175.8 0.0 copy-done.2
  175.8 2.7 %fusion.22 = f32[2,256,256]{1,2,0:T(8,128)S(1)} fusion(f32[256,2,1024]{2,0,1:T(8,128)S(1)} %copy-done.2, f32[256,2,1024]{2,0,1:T(8,128)} %fusion, bf16[1024,256]{1,0:T(8,128)(2,1)S(1)} %copy-done), kind=kOutput, calls=%fused_computation.20 | convolution fusion | flops 1611137024 | bytes 5242880 | tf_op jit(solution)/shard_map/gb,fgc->fbc/dot_general | solution.py:38
  178.6 0.0 copy-done.3
  178.6 0.0 copy-done.4
  178.7 0.9 fusion.28
  179.6 0.0 reduce-scatter.2.cloned.1.call-update
  179.6 0.0 copy-done.5
  179.6 0.6 dynamic-slice
  180.9 15.3 %reduce-scatter.2.cloned.1.call-done = f32[32,256]{1,0:T(8,128)} async-done(((f32[128,256]{1,0:T(8,128)}), f32[32,256]{1,0:T(8,128)}) %reduce-scatter.2.cloned.1.call-update) | async-done | bytes 32784 | tf_op jit(solution)/shard_map/reduce_scatter | solution.py:49
  196.2 37.8 %all-reduce = f32[32,256]{1,0:T(8,128)S(1)} all-reduce(f32[32,256]{1,0:T(8,128)} %reduce-scatter.2.cloned.1.call-done), channel_id=3, replica_groups=mesh['freq'=4,'gblk'=8] {'gblk'}, use_global_device_ids=true, to_apply=%region_2.3.clone | all-reduce | flops 8192 | bytes 65536
  233.9 0.6 constant_dynamic-slice_fusion
  (14 shorter events, 0.5 us)
Async XLA Ops:
  6.5 106.8 %copy-start = (bf16[1024,256]{1,0:T(8,128)(2,1)S(1)}, bf16[1024,256]{1,0:T(8,128)(2,1)}, u32[]{:S(2)}) copy-start(bf16[1024,256]{1,0:T(8,128)(2,1)} %param.8) | copy-start | bytes 1572868
  6.5 189.6 %reduce-scatter.2.cloned.1.call-start = ((), (), s32[]{:S(2)}) async-start(), calls=%async_computation.1 | async-start | bytes 163840 | tf_op jit(solution)/shard_map/reduce_scatter | solution.py:49
  6.5 18.2 %collective-permute-start = (bf16[1024,256]{1,0:T(8,128)(2,1)}, bf16[1024,256]{1,0:T(8,128)(2,1)S(1)}, u32[]{:S(2)}, u32[]{:S(2)}) collective-permute-start(bf16[1024,256]{1,0:T(8,128)(2,1)} %param.8), channel_id=1, source_target_pairs={{0,1},{1,2},{2,3},{3,4},{4,5},{5,6},{6,7},{7,0},{8,9},{9,10},{10,1... | collective-permute-start | bytes 1572872 | tf_op jit(solution)/shard_map/ppermute | solution.py:17
  24.8 15.8 %collective-permute-start.1 = (bf16[1024,256]{1,0:T(8,128)(2,1)S(1)}, bf16[1024,256]{1,0:T(8,128)(2,1)S(1)}, u32[]{:S(2)}, u32[]{:S(2)}) collective-permute-start(bf16[1024,256]{1,0:T(8,128)(2,1)S(1)} %collective-permute-done), channel_id=1, source_target_pairs={{0,1},{1,2},{2,3},{3,4},{4,5},{5,6},{6,7},{7,0},{8,9},{9,10},{10,1... | collective-permute-start | bytes 1572872 | tf_op jit(solution)/shard_map/ppermute | solution.py:17
  40.6 14.9 %collective-permute-start.2 = (bf16[1024,256]{1,0:T(8,128)(2,1)S(1)}, bf16[1024,256]{1,0:T(8,128)(2,1)S(1)}, u32[]{:S(2)}, u32[]{:S(2)}) collective-permute-start(bf16[1024,256]{1,0:T(8,128)(2,1)S(1)} %collective-permute-done.1), channel_id=1, source_target_pairs={{0,1},{1,2},{2,3},{3,4},{4,5},{5,6},{6,7},{7,0},{8,9},{9,10},{10,1... | collective-permute-start | bytes 1572872 | tf_op jit(solution)/shard_map/ppermute | solution.py:17
  55.5 14.1 %collective-permute-start.3 = (bf16[1024,256]{1,0:T(8,128)(2,1)S(1)}, bf16[1024,256]{1,0:T(8,128)(2,1)S(1)}, u32[]{:S(2)}, u32[]{:S(2)}) collective-permute-start(bf16[1024,256]{1,0:T(8,128)(2,1)S(1)} %collective-permute-done.2), channel_id=1, source_target_pairs={{0,1},{1,2},{2,3},{3,4},{4,5},{5,6},{6,7},{7,0},{8,9},{9,10},{10,1... | collective-permute-start | bytes 1572872 | tf_op jit(solution)/shard_map/ppermute | solution.py:17
  69.6 13.2 %collective-permute-start.4 = (bf16[1024,256]{1,0:T(8,128)(2,1)S(1)}, bf16[1024,256]{1,0:T(8,128)(2,1)S(1)}, u32[]{:S(2)}, u32[]{:S(2)}) collective-permute-start(bf16[1024,256]{1,0:T(8,128)(2,1)S(1)} %collective-permute-done.3), channel_id=1, source_target_pairs={{0,1},{1,2},{2,3},{3,4},{4,5},{5,6},{6,7},{7,0},{8,9},{9,10},{10,1... | collective-permute-start | bytes 1572872 | tf_op jit(solution)/shard_map/ppermute | solution.py:17
  82.8 12.5 %collective-permute-start.5 = (bf16[1024,256]{1,0:T(8,128)(2,1)S(1)}, bf16[1024,256]{1,0:T(8,128)(2,1)}, u32[]{:S(2)}, u32[]{:S(2)}) collective-permute-start(bf16[1024,256]{1,0:T(8,128)(2,1)S(1)} %collective-permute-done.4), channel_id=1, source_target_pairs={{0,1},{1,2},{2,3},{3,4},{4,5},{5,6},{6,7},{7,0},{8,9},{9,10},{10,1... | collective-permute-start | bytes 1572872 | tf_op jit(solution)/shard_map/ppermute | solution.py:17
  95.2 12.2 %collective-permute-start.6 = (bf16[1024,256]{1,0:T(8,128)(2,1)}, bf16[1024,256]{1,0:T(8,128)(2,1)}, u32[]{:S(2)}, u32[]{:S(2)}) collective-permute-start(bf16[1024,256]{1,0:T(8,128)(2,1)} %collective-permute-done.5), channel_id=1, source_target_pairs={{0,1},{1,2},{2,3},{3,4},{4,5},{5,6},{6,7},{7,0},{8,9},{9,10},{10,1... | collective-permute-start | bytes 1572872 | tf_op jit(solution)/shard_map/ppermute | solution.py:17
  113.3 19.1 %copy-start.1 = (bf16[16384,256]{1,0:T(8,128)(2,1)}, bf16[16384,256]{1,0:T(8,128)(2,1)S(1)}, u32[]{:S(2)}) copy-start(bf16[16384,256]{1,0:T(8,128)(2,1)S(1)} %constant_dynamic-update-slice_fusion) | copy-start | bytes 25165828
  161.0 14.8 %copy-start.2 = (f32[256,2,1024]{2,0,1:T(8,128)S(1)}, f32[256,2,1024]{2,0,1:T(8,128)}, u32[]{:S(2)}) copy-start(f32[256,2,1024]{2,0,1:T(8,128)} %fusion.2) | copy-start | bytes 6291460
  161.0 17.6 %copy-start.3 = (f32[2,128]{1,0:T(2,128)S(1)}, f32[2,128]{1,0:T(2,128)}, u32[]{:S(2)}) copy-start(f32[2,128]{1,0:T(2,128)} %param.9) | copy-start | bytes 3076
  173.9 4.7 %copy-start.4 = (s32[128]{0:T(128)S(1)}, s32[128]{0:T(128)}, u32[]{:S(2)}) copy-start(s32[128]{0:T(128)} %param.11) | copy-start | bytes 1540
  173.9 5.7 %copy-start.5 = (u32[32]{0:T(128)S(1)}, u32[32]{0:T(128)}, u32[]{:S(2)}) copy-start(u32[32]{0:T(128)} %constant.41) | copy-start | bytes 388
Sparse Core Ops, SparseCore 0:
  179.7 16.3 reduce-scatter.1
